TPU v7x, 32 devices: a whole 2x2x4 slice. The times are simulated.
32 devices in a mesh: space: 8 (over z, y), level: 4 (over x, core).
Axes of the slice: x: 2, y: 2, z: 4, core: 2. Of those that a mesh axis runs over, the one named last changes fastest.
Arguments:
- grid_latent: bfloat16 [4096, 512], P('space'), may hold values from -6 to 6
- mesh_latent: bfloat16 [4, 64, 512], P('level', 'space'), may hold values from -6 to 6
- grid_output_cotangent: bfloat16 [4096, 512], P('space'), may hold values from -6 to 6
- w_send: bfloat16 [512, 512], replicated, may hold values from -0.25 to 0.25
- w_recv: bfloat16 [512, 512], replicated, may hold values from -0.25 to 0.25
- output_weight: bfloat16 [512, 512], replicated, may hold values from -0.25 to 0.25
- hidden_layer_bias: float32 [512], replicated, may hold values from -4 to 4
- output_norm_gain: float32 [512], replicated, may hold values from 0.1 to 1.9
- edge_sender: int32 [4, 16384], P('level', 'space'), may hold values from 0 to 23
- edge_receiver: int32 [4, 16384], P('level', 'space'), may hold values from 0 to 511
- edge_live: int32 [4, 16384], P('level', 'space'), may hold values 0 or 1
Outputs:
- d_grid: float32 [4096, 512], P(('space', 'level'))
- d_mesh: float32 [4, 64, 512], P('level', 'space')
- d_w_send: bfloat16 [512, 512], replicated
- d_w_recv: bfloat16 [512, 512], replicated
- d_w_out: bfloat16 [512, 512], replicated
- d_bias: float32 [512], replicated
- d_gain: float32 [512], replicated
All inputs are finite; a program needn't handle non-finite values. No bound on the sum of `edge_live` on one device may be relied on, other than what follows from the above.
Results may differ from a plain program's by a relative error of at most 0.012.
Values may be sent and summed in bfloat16 or wider, within the bound.
No kernel may reach another device: no remote copies, remote signals or barrier semaphores. Data moves between devices by JAX's collectives and lax.ppermute only.
A program may use at most 64 MiB of HBM per device.

v0:
```python
import jax
import jax.numpy as jnp
from jax import lax
from jax.sharding import PartitionSpec as P


def with_halo(cells, sides, width):
    for axis, dim in sides:
        count = lax.axis_size(axis)
        ends = count - 1
        head = lax.slice_in_dim(cells, 0, width, axis=dim)
        tail = lax.slice_in_dim(cells, cells.shape[dim] - width, cells.shape[dim], axis=dim)
        cells = jnp.concatenate(
            [
                lax.ppermute(tail, axis, [(i, (i + 1) % count) for i in range(ends)]),
                cells,
                lax.ppermute(head, axis, [((i + 1) % count, i) for i in range(ends)]),
            ],
            axis=dim,
        )
    return cells


def from_behind(block, axis, distance):
    devices = range(lax.axis_size(axis))
    route = [(i - distance, i) for i in devices if i - distance in devices]
    return lax.ppermute(block, axis, route)


def edge_reverse_step(
    sending_rows,
    receiver_rows,
    cotangent_lines,
    slot_active_flags,
    output_weight,
    hidden_layer_bias,
    output_norm_gain,
):
    preact = sending_rows + receiver_rows + hidden_layer_bias
    hidden = jax.nn.silu(preact).astype(jnp.bfloat16)
    outer = jnp.dot(hidden, output_weight, preferred_element_type=jnp.float32)
    center = outer - jnp.mean(outer, axis=-1, keepdims=True)
    inv_scale = lax.rsqrt(jnp.mean(center * center, axis=-1, keepdims=True) + 1e-05)
    normed = center * inv_scale
    incoming_gradient = cotangent_lines.astype(jnp.float32) * slot_active_flags[:, None].astype(
        jnp.float32
    )
    scaled = incoming_gradient * output_norm_gain
    d_outer = inv_scale * (
        scaled
        - jnp.mean(scaled, axis=-1, keepdims=True)
        - normed * jnp.mean(scaled * normed, axis=-1, keepdims=True)
    )
    d_outer_b = d_outer.astype(jnp.bfloat16)
    w_out_grad = jnp.dot(hidden.T, d_outer_b, preferred_element_type=jnp.float32)
    d_hidden = jnp.dot(d_outer_b, output_weight.T, preferred_element_type=jnp.float32)
    sigmoid = jax.nn.sigmoid(preact)
    preactivation_gradient = d_hidden * sigmoid * (1.0 + preact * (1.0 - sigmoid))
    return (
        preactivation_gradient,
        w_out_grad,
        jnp.sum(preactivation_gradient, axis=0),
        jnp.sum(incoming_gradient * normed, axis=0),
    )


def body(
    grid_latent,
    mesh_latent,
    grid_output_cotangent,
    w_send,
    w_recv,
    output_weight,
    hidden_layer_bias,
    output_norm_gain,
    edge_sender,
    edge_receiver,
    edge_live,
):
    shards = lax.axis_size("space")
    width = grid_latent.shape[1]
    grid_rows = grid_latent.shape[0]
    mesh_rows = mesh_latent.shape[1]
    slots = edge_sender.shape[1]
    sender_local = edge_sender[0]
    receiver_index = edge_receiver[0]
    band = lax.axis_index("space")
    window = sender_local // mesh_rows
    target = band + window - 1
    inside = (target >= 0) & (target < shards)
    window = jnp.where(inside, window, 1)
    table_row = window * mesh_rows + sender_local % mesh_rows
    proj_send = jnp.dot(mesh_latent[0], w_send, preferred_element_type=jnp.float32).astype(
        jnp.bfloat16
    )
    projected_receiver = jnp.dot(grid_latent, w_recv, preferred_element_type=jnp.float32)
    table = with_halo(proj_send, (("space", 0),), mesh_rows)
    sending_rows = table[table_row]
    block = 512
    blocks = slots // block

    def run_block(operands):
        rows_send, rows_recv, rows_cot, rows_live = operands
        return edge_reverse_step(
            rows_send.astype(jnp.float32),
            rows_recv,
            rows_cot,
            rows_live,
            output_weight,
            hidden_layer_bias,
            output_norm_gain,
        )

    operands = (
        sending_rows.reshape(blocks, block, width),
        projected_receiver[receiver_index].reshape(blocks, block, width),
        grid_output_cotangent[receiver_index].reshape(blocks, block, width),
        edge_live[0].reshape(blocks, block),
    )
    d_pre_blocks, wout_blocks, bias_blocks, gain_blocks = lax.map(run_block, operands)
    preactivation_gradient = d_pre_blocks.reshape(slots, width)
    output_weight_piece = jnp.sum(wout_blocks, axis=0)
    bias_piece = jnp.sum(bias_blocks, axis=0)
    gain_piece = jnp.sum(gain_blocks, axis=0)
    table_grads = jax.ops.segment_sum(preactivation_gradient, table_row, num_segments=3 * mesh_rows)
    below = table_grads[:mesh_rows]
    above = table_grads[2 * mesh_rows :]
    from_below = from_behind(above, "space", 1)
    from_above = from_behind(below, "space", -1)
    mesh_acc = table_grads[mesh_rows : 2 * mesh_rows] + from_below + from_above
    grid_local = jax.ops.segment_sum(preactivation_gradient, receiver_index, num_segments=grid_rows)
    share = grid_rows // lax.axis_size("level")
    offset = lax.axis_index("level") * share
    grid_acc = lax.psum_scatter(
        grid_local.astype(jnp.bfloat16), "level", scatter_dimension=0, tiled=True
    )
    grid_part = lax.dynamic_slice_in_dim(grid_latent, offset, share, 0)
    mesh_sum = mesh_acc.astype(jnp.bfloat16)
    d_mesh = jnp.dot(mesh_sum, w_send.T, preferred_element_type=jnp.float32)[None]
    d_grid = jnp.dot(grid_acc, w_recv.T, preferred_element_type=jnp.float32)
    wsend_part = jnp.dot(mesh_latent[0].T, mesh_sum, preferred_element_type=jnp.float32)
    wrecv_part = jnp.dot(grid_part.T, grid_acc, preferred_element_type=jnp.float32)
    totals = lax.psum(
        (wsend_part, wrecv_part, output_weight_piece, bias_piece, gain_piece), ("space", "level")
    )
    d_w_send = totals[0].astype(jnp.bfloat16)
    d_w_recv = totals[1].astype(jnp.bfloat16)
    d_w_out = totals[2].astype(jnp.bfloat16)
    d_bias = totals[3]
    d_gain = totals[4]
    return (d_grid, d_mesh, d_w_send, d_w_recv, d_w_out, d_bias, d_gain)


def solution(mesh):
    return jax.shard_map(
        body,
        mesh=mesh,
        in_specs=(
            P("space", None),
            P("level", "space", None),
            P("space", None),
            P(),
            P(),
            P(),
            P(),
            P(),
            P("level", "space"),
            P("level", "space"),
            P("level", "space"),
        ),
        out_specs=(P(("space", "level"), None), P("level", "space", None), P(), P(), P(), P(), P()),
        check_vma=False,
    )
```

profile of v0, /device:TPU:0, one launch (start us, length us, event | category | flops | bytes accessed | tf_op | source)
XLA Modules:
  0.0 218.6 jit_solution(9644242598406611209)
XLA Ops:
  9.8 5.5 %collective-permute-start = (bf16[8,512]{1,0:T(8,128)(2,1)S(1)}, bf16[8,512]{1,0:T(8,128)(2,1)S(1)}, u32[]{:S(2)}, u32[]{:S(2)}) collective-permute-start(bf16[8,512]{1,0:T(8,128)(2,1)S(1)} %convolution_convert_fusion), channel_id=1, source_target_pairs={{0,4},{4,8},{8,12},{12,16},{16,20},{20,24},{24,28},{1,5},{5,9},{9,... | collective-permute-start | bytes 24584 | tf_op jit(solution)/shard_map/ppermute | solution.py:15
  16.9 1.6 fusion.27
  20.5 9.2 %gather_fusion.2 = bf16[2048,512]{1,0:T(8,128)(2,1)} fusion(bf16[512,512]{1,0:T(8,128)(2,1)S(1)} %copy-done, s32[2048]{0:T(1024)S(1)} %broadcast_clamp_fusion), kind=kCustom, calls=%fused_computation.2 | custom fusion | bytes 4202496 | tf_op jit(solution)/shard_map/gather | solution.py:117
  29.6 8.9 %gather_fusion.1 = f32[2048,512]{1,0:T(8,128)} fusion(f32[512,512]{1,0:T(8,128)S(1)} %fusion.27, s32[2048]{0:T(1024)S(1)} %broadcast_clamp_fusion), kind=kCustom, calls=%fused_computation.1 | custom fusion | bytes 8396800 | tf_op jit(solution)/shard_map/gather | solution.py:116
  38.6 9.2 %gather_fusion = bf16[2048,512]{1,0:T(8,128)(2,1)} fusion(bf16[24,512]{1,0:T(8,128)(2,1)S(1)} %pad_maximum_fusion, s32[2048]{0:T(1024)S(1)} %broadcast_clamp_fusion.1), kind=kCustom, calls=%fused_computation | custom fusion | bytes 4202496 | tf_op jit(solution)/shard_map/gather | solution.py:98
  47.8 37.2 %while.16 = (s32[]{:T(128)}, f32[4,512,512]{2,1,0:T(8,128)}, f32[4,512,512]{2,1,0:T(8,128)}, f32[4,512]{1,0:T(4,128)S(1)}, f32[4,512]{1,0:T(4,128)S(1)}, /*index...) while((s32[]{:T(128)}, f32[4,512,512]{2,1,0:T(8,128)}, ...), condition=%wide.region_7.8_spmd, body=%wide.region_0.7_spmd.sunk | while | flops 816840704 | bytes 18942132 | solution.py:120
  47.8 1.7 multiply_convert_fusion.2
  52.3 1.6 fusion.63
  53.9 3.0 %bitcast_dynamic-update-slice_fusion.2 = (f32[4,512,512]{2,1,0:T(8,128)}, f32[512,512]{1,0:T(8,128)S(1)}) fusion(f32[4,512,512]{2,1,0:T(8,128)} %get-tuple-element.263, s32[]{:T(128)S(6)} %copy.34, f32[512]{0:T(512)S(1)} %get-tuple-element.284, f32[4,512,512]{2,1,0:T(8,128)} %get-tuple-element.283, bf16[4,512,512]{2,1,0:T(8,128)(2,1)} %get-tuple-element.282, ...), kind=kOutput, calls=%fused_computation.20.clone.1 | convolution fusion | flops 271319040 | bytes 4720644 | tf_op jit(solution)/shard_map/while/body/eval_jaxpr/dot_general | solution.py:56
  57.1 1.7 multiply_convert_fusion.2
  61.7 1.5 fusion.63
  63.2 3.1 %bitcast_dynamic-update-slice_fusion.2 = (f32[4,512,512]{2,1,0:T(8,128)}, f32[512,512]{1,0:T(8,128)S(1)}) fusion(f32[4,512,512]{2,1,0:T(8,128)} %get-tuple-element.263, s32[]{:T(128)S(6)} %copy.34, f32[512]{0:T(512)S(1)} %get-tuple-element.284, f32[4,512,512]{2,1,0:T(8,128)} %get-tuple-element.283, bf16[4,512,512]{2,1,0:T(8,128)(2,1)} %get-tuple-element.282, ...), kind=kOutput, calls=%fused_computation.20.clone.1 | convolution fusion | flops 271319040 | bytes 4720644 | tf_op jit(solution)/shard_map/while/body/eval_jaxpr/dot_general | solution.py:56
  66.4 1.7 multiply_convert_fusion.2
  71.0 1.5 fusion.63
  72.5 3.1 %bitcast_dynamic-update-slice_fusion.2 = (f32[4,512,512]{2,1,0:T(8,128)}, f32[512,512]{1,0:T(8,128)S(1)}) fusion(f32[4,512,512]{2,1,0:T(8,128)} %get-tuple-element.263, s32[]{:T(128)S(6)} %copy.34, f32[512]{0:T(512)S(1)} %get-tuple-element.284, f32[4,512,512]{2,1,0:T(8,128)} %get-tuple-element.283, bf16[4,512,512]{2,1,0:T(8,128)(2,1)} %get-tuple-element.282, ...), kind=kOutput, calls=%fused_computation.20.clone.1 | convolution fusion | flops 271319040 | bytes 4720644 | tf_op jit(solution)/shard_map/while/body/eval_jaxpr/dot_general | solution.py:56
  75.7 1.7 multiply_convert_fusion.2
  81.7 3.0 %bitcast_dynamic-update-slice_fusion.2 = (f32[4,512,512]{2,1,0:T(8,128)}, f32[512,512]{1,0:T(8,128)S(1)}) fusion(f32[4,512,512]{2,1,0:T(8,128)} %get-tuple-element.263, s32[]{:T(128)S(6)} %copy.34, f32[512]{0:T(512)S(1)} %get-tuple-element.284, f32[4,512,512]{2,1,0:T(8,128)} %get-tuple-element.283, bf16[4,512,512]{2,1,0:T(8,128)(2,1)} %get-tuple-element.282, ...), kind=kOutput, calls=%fused_computation.20.clone.1 | convolution fusion | flops 271319040 | bytes 4720644 | tf_op jit(solution)/shard_map/while/body/eval_jaxpr/dot_general | solution.py:56
  84.9 13.5 %scatter_custom_fusion = f32[512,512]{1,0:T(8,128)S(1)} fusion(s32[2048]{0:T(1024)} %bitcast.107, f32[2048,512]{1,0:T(8,128)} %bitcast.108, f32[]{:T(128)} %constant.75.clone.1), kind=kCustom, calls=%fused_computation.35 | custom fusion | flops 1048576 | bytes 1049088 | tf_op jit(solution)/shard_map/scatter-add | solution.py:131
  99.3 13.2 %scatter_custom_fusion.1 = f32[24,512]{1,0:T(8,128)S(1)} fusion(s32[2048]{0:T(1024)S(1)} %bitcast.106, f32[2048,512]{1,0:T(8,128)} %bitcast.109, f32[]{:T(128)} %constant.75.clone.1), kind=kCustom, calls=%fused_computation.45 | custom fusion | flops 1048576 | bytes 49664 | tf_op jit(solution)/shard_map/scatter-add | solution.py:125
  112.6 4.8 %collective-permute-start.2 = (f32[8,512]{1,0:T(8,128)S(1)}, f32[8,512]{1,0:T(8,128)S(1)}, u32[]{:S(2)}, u32[]{:S(2)}) collective-permute-start(f32[8,512]{1,0:T(8,128)S(1)} %get-tuple-element.154), channel_id=1, source_target_pairs={{0,4},{4,8},{8,12},{12,16},{16,20},{20,24},{24,28},{1,5},{5,9},{9,... | collective-permute-start | bytes 49160 | tf_op jit(solution)/shard_map/ppermute | solution.py:27
  117.4 1.5 collective-permute-start.3
  118.9 3.8 %reduce_sum.81 = f32[512,512]{1,0:T(8,128)} reduce(f32[4,512,512]{2,1,0:T(8,128)} %get-tuple-element.73, f32[]{:T(128)} %constant.75.clone.1), dimensions={0}, to_apply=%region_13.14 | reduce | flops 786432 | bytes 5242884 | tf_op jit(solution)/shard_map/reduce_sum | solution.py:122
  125.6 83.1 %all-reduce.2 = (bf16[512,512]{0,1:T(8,128)(2,1)}, bf16[512,512]{1,0:T(8,128)(2,1)}, bf16[512,512]{1,0:T(8,128)(2,1)}, f32[512]{0:T(512)}, f32[512]{0:T(512)}) all-reduce(f32[512,512]{0,1:T(8,128)S(1)} %convolution_bitcast_fusion.1, f32[512,512]{1,0:T(8,128)S(1)} %fusion.14, ...), channel_id=1, replica_groups=mesh['space'=8,'level'=4] {'space','level'}, use_global_device_ids=true, to_apply=%region_11.12 | all-reduce | flops 787456 | bytes 4726784 | tf_op jit(solution)/shard_map/psum | solution.py:143
  208.7 2.0 copy.21
  (99 shorter events, 24.4 us)
Async XLA Ops:
  7.2 13.3 %copy-start = (bf16[512,512]{1,0:T(8,128)(2,1)S(1)}, bf16[512,512]{1,0:T(8,128)(2,1)}, u32[]{:S(2)}) copy-start(bf16[512,512]{1,0:T(8,128)(2,1)} %param.15) | copy-start | bytes 1572868
  7.2 117.1 %reduce-scatter.2.cloned.1.call-start = ((), (), s32[]{:S(2)}) async-start(), calls=%async_computation.1 | async-start | bytes 655360 | tf_op jit(solution)/shard_map/reduce_scatter | solution.py:134
  8.5 30.0 %collective-permute-start.1 = (bf16[8,512]{1,0:T(8,128)(2,1)S(1)}, bf16[8,512]{1,0:T(8,128)(2,1)S(1)}, u32[]{:S(2)}, u32[]{:S(2)}) collective-permute-start(bf16[8,512]{1,0:T(8,128)(2,1)S(1)} %convolution_convert_fusion), channel_id=1, source_target_pairs={{4,0},{8,4},{12,8},{16,12},{20,16},{24,20},{28,24},{5,1},{9,5},{13... | collective-permute-start | bytes 24584 | tf_op jit(solution)/shard_map/ppermute | solution.py:17
  9.8 28.7 %collective-permute-start = (bf16[8,512]{1,0:T(8,128)(2,1)S(1)}, bf16[8,512]{1,0:T(8,128)(2,1)S(1)}, u32[]{:S(2)}, u32[]{:S(2)}) collective-permute-start(bf16[8,512]{1,0:T(8,128)(2,1)S(1)} %convolution_convert_fusion), channel_id=1, source_target_pairs={{0,4},{4,8},{8,12},{12,16},{16,20},{20,24},{24,28},{1,5},{5,9},{9,... | collective-permute-start | bytes 24584 | tf_op jit(solution)/shard_map/ppermute | solution.py:15
  38.5 9.2 %copy-start.1 = (bf16[512,512]{1,0:T(8,128)(2,1)S(1)}, bf16[512,512]{1,0:T(8,128)(2,1)}, u32[]{:S(2)}) copy-start(bf16[512,512]{1,0:T(8,128)(2,1)} %param.18) | copy-start | bytes 1572868
  38.5 9.2 %copy-start.5 = (f32[512]{0:T(512)S(1)}, f32[512]{0:T(512)}, u32[]{:S(2)}) copy-start(f32[512]{0:T(512)} %param.20) | copy-start | bytes 6148
  38.5 9.2 %copy-start.6 = (f32[512]{0:T(512)S(1)}, f32[512]{0:T(512)}, u32[]{:S(2)}) copy-start(f32[512]{0:T(512)} %param.19) | copy-start | bytes 6148
  84.9 38.1 %copy-start.7 = (bf16[1,8,512]{2,1,0:T(8,128)(2,1)S(1)}, bf16[1,8,512]{2,1,0:T(8,128)(2,1)}, u32[]{:S(2)}) copy-start(bf16[1,8,512]{2,1,0:T(8,128)(2,1)} %param.14) | copy-start | bytes 24580
  98.4 25.0 %copy-start.2 = (bf16[512,512]{1,0:T(8,128)(2,1)S(1)}, bf16[512,512]{1,0:T(8,128)(2,1)}, u32[]{:S(2)}) copy-start(bf16[512,512]{1,0:T(8,128)(2,1)} %param.16) | copy-start | bytes 1572868
  112.6 10.1 %collective-permute-start.2 = (f32[8,512]{1,0:T(8,128)S(1)}, f32[8,512]{1,0:T(8,128)S(1)}, u32[]{:S(2)}, u32[]{:S(2)}) collective-permute-start(f32[8,512]{1,0:T(8,128)S(1)} %get-tuple-element.154), channel_id=1, source_target_pairs={{0,4},{4,8},{8,12},{12,16},{16,20},{20,24},{24,28},{1,5},{5,9},{9,... | collective-permute-start | bytes 49160 | tf_op jit(solution)/shard_map/ppermute | solution.py:27
  117.4 5.6 %collective-permute-start.3 = (f32[8,512]{1,0:T(8,128)S(1)}, f32[8,512]{1,0:T(8,128)S(1)}, u32[]{:S(2)}, u32[]{:S(2)}) collective-permute-start(f32[8,512]{1,0:T(8,128)S(1)} %get-tuple-element.155), channel_id=1, source_target_pairs={{4,0},{8,4},{12,8},{16,12},{20,16},{24,20},{28,24},{5,1},{9,5},{13... | collective-permute-start | bytes 49160 | tf_op jit(solution)/shard_map/ppermute | solution.py:27
  122.7 88.0 %copy-start.3 = (bf16[512,512]{1,0:T(8,128)(2,1)S(1)}, bf16[512,512]{1,0:T(8,128)(2,1)}, u32[]{:S(2)}) copy-start(bf16[512,512]{1,0:T(8,128)(2,1)} %param.17) | copy-start | bytes 1572868
  124.3 86.5 %copy-start.4 = (bf16[128,512]{1,0:T(8,128)(2,1)S(1)}, bf16[128,512]{1,0:T(8,128)(2,1)}, u32[]{:S(2)}) copy-start(bf16[128,512]{1,0:T(8,128)(2,1)} %reduce-scatter.2.cloned.1.call-done) | copy-start | bytes 393220
Sparse Core Ops, SparseCore 0:
  99.4 23.2 reduce-scatter.1
where the time goes:
time: 220 us; the launch traced here: 219 us
  blocking collectives  83.1 us (38%)
  other arithmetic  45.5 us (21%)
  local copies, waits for them, and re-layouts  35.4 us (16%)
  matrix products  26.6 us (12%)
  between operations  14.3 us (6%)
  starting transfers between devices  13.2 us (6%)
    psum x1, blocking collectives, body(): lax.psum((wsend_part, wrecv_part, output_weight_piece, bias_piece, gain_p...  83.1 us
    scatter-add x1, other arithmetic, body(): jax.ops.segment_sum(preactivation_gradient, receiver_index, num_segments=...  13.5 us
    scatter-add x1, other arithmetic, body(): jax.ops.segment_sum(preactivation_gradient, table_row, num_segments=3 * m...  13.2 us
    dot_general x4, matrix products, edge_reverse_step(): jnp.dot(d_outer_b, output_weight.T, preferred_element_type=jnp.float32)  12.2 us
    gather x1, local copies, waits for them, and re-layouts, body(): sending_rows = table[table_row]  9.18 us
    gather x1, local copies, waits for them, and re-layouts, body(): grid_output_cotangent[receiver_index].reshape(blocks, block, width)  9.15 us
    gather x1, local copies, waits for them, and re-layouts, body(): projected_receiver[receiver_index].reshape(blocks, block, width)  8.9 us
    convert_element_type x4, other arithmetic, edge_reverse_step(): hidden = jax.nn.silu(preact).astype(jnp.bfloat16)  6.68 us
  transfers between devices with their start and end apart: 5, of which 1 were waited for; matrix products, arithmetic and copies ran while one was open for 19% of the time, Pallas kernels for 0%

commit v1 on v0

--- a/solution.py
+++ b/solution.py
@@ -141,7 +141,8 @@
     wsend_part = jnp.dot(mesh_latent[0].T, mesh_sum, preferred_element_type=jnp.float32)
     wrecv_part = jnp.dot(grid_part.T, grid_acc, preferred_element_type=jnp.float32)
     totals = lax.psum(
-        (wsend_part, wrecv_part, output_weight_piece, bias_piece, gain_piece), ("space", "level")
+        lax.psum((wsend_part, wrecv_part, output_weight_piece, bias_piece, gain_piece), "level"),
+        "space",
     )
     d_w_send = totals[0].astype(jnp.bfloat16)
     d_w_recv = totals[1].astype(jnp.bfloat16)

time: 220 us -> 336 us (1.53)
  waiting for transfers between devices: 0.36 us -> 62.6 us
  blocking collectives: 83.1 us -> 136 us
    psum x0 -> x1, blocking collectives: none -> 131 us  [body(): lax.psum(lax.psum((wsend_part, wrecv_part, output_weight_piece, bias_piec...]
    psum x1, blocking collectives: 83.1 us -> 5.66 us  [body(): lax.psum((wsend_part, wrecv_part, output_weight_piece, bias_piece, gain_p...]
    psum x0 -> x1, waiting for transfers between devices: none -> 62.2 us  [body(): lax.psum((wsend_part, wrecv_part, output_weight_piece, bias_piece, gain_p...]
  transfers between devices with their start and end apart: 5 -> 6, of which waited for: 1 -> 2; matrix products, arithmetic and copies ran while one was open for 19% -> 13% of each run, Pallas kernels for 0% -> 0%
where the time goes in v1:
time: 336 us; the launch traced here: 335 us
  blocking collectives  136 us (40%)
  waiting for transfers between devices  62.6 us (19%)
  other arithmetic  45.5 us (14%)
  local copies, waits for them, and re-layouts  34.4 us (10%)
  matrix products  28.6 us (9%)
  between operations  14.3 us (4%)
  starting transfers between devices  13.2 us (4%)
    psum x1, blocking collectives, body(): lax.psum(lax.psum((wsend_part, wrecv_part, output_weight_piece, bias_piec...  131 us
    psum x1, waiting for transfers between devices, body(): lax.psum((wsend_part, wrecv_part, output_weight_piece, bias_piece, gain_p...  62.2 us
    scatter-add x1, other arithmetic, body(): jax.ops.segment_sum(preactivation_gradient, receiver_index, num_segments=...  13.5 us
    scatter-add x1, other arithmetic, body(): jax.ops.segment_sum(preactivation_gradient, table_row, num_segments=3 * m...  13.2 us
    dot_general x4, matrix products, edge_reverse_step(): jnp.dot(d_outer_b, output_weight.T, preferred_element_type=jnp.float32)  12.2 us
    gather x1, local copies, waits for them, and re-layouts, body(): sending_rows = table[table_row]  9.18 us
    gather x1, local copies, waits for them, and re-layouts, body(): grid_output_cotangent[receiver_index].reshape(blocks, block, width)  9.15 us
    gather x1, local copies, waits for them, and re-layouts, body(): projected_receiver[receiver_index].reshape(blocks, block, width)  8.9 us
  transfers between devices with their start and end apart: 6, of which 2 were waited for; matrix products, arithmetic and copies ran while one was open for 13% of the time, Pallas kernels for 0%

profile of v1, /device:TPU:0, one launch (start us, length us, event | category | flops | bytes accessed | tf_op | source)
XLA Modules:
  0.0 334.9 jit_solution(3485178069087858192)
XLA Ops:
  9.8 5.5 %collective-permute-start = (bf16[8,512]{1,0:T(8,128)(2,1)S(1)}, bf16[8,512]{1,0:T(8,128)(2,1)S(1)}, u32[]{:S(2)}, u32[]{:S(2)}) collective-permute-start(bf16[8,512]{1,0:T(8,128)(2,1)S(1)} %convolution_convert_fusion), channel_id=1, source_target_pairs={{0,4},{4,8},{8,12},{12,16},{16,20},{20,24},{24,28},{1,5},{5,9},{9,... | collective-permute-start | bytes 24584 | tf_op jit(solution)/shard_map/ppermute | solution.py:15
  16.9 1.6 fusion.27
  20.5 9.2 %gather_fusion.2 = bf16[2048,512]{1,0:T(8,128)(2,1)} fusion(bf16[512,512]{1,0:T(8,128)(2,1)S(1)} %copy-done, s32[2048]{0:T(1024)S(1)} %broadcast_clamp_fusion), kind=kCustom, calls=%fused_computation.2 | custom fusion | bytes 4202496 | tf_op jit(solution)/shard_map/gather | solution.py:117
  29.6 8.9 %gather_fusion.1 = f32[2048,512]{1,0:T(8,128)} fusion(f32[512,512]{1,0:T(8,128)S(1)} %fusion.27, s32[2048]{0:T(1024)S(1)} %broadcast_clamp_fusion), kind=kCustom, calls=%fused_computation.1 | custom fusion | bytes 8396800 | tf_op jit(solution)/shard_map/gather | solution.py:116
  38.6 9.2 %gather_fusion = bf16[2048,512]{1,0:T(8,128)(2,1)} fusion(bf16[24,512]{1,0:T(8,128)(2,1)S(1)} %pad_maximum_fusion, s32[2048]{0:T(1024)S(1)} %broadcast_clamp_fusion.1), kind=kCustom, calls=%fused_computation | custom fusion | bytes 4202496 | tf_op jit(solution)/shard_map/gather | solution.py:98
  47.8 37.2 %while.16 = (s32[]{:T(128)}, f32[4,512,512]{2,1,0:T(8,128)}, f32[4,512,512]{2,1,0:T(8,128)}, f32[4,512]{1,0:T(4,128)S(1)}, f32[4,512]{1,0:T(4,128)S(1)}, /*index...) while((s32[]{:T(128)}, f32[4,512,512]{2,1,0:T(8,128)}, ...), condition=%wide.region_7.8_spmd, body=%wide.region_0.7_spmd.sunk | while | flops 816840704 | bytes 18942132 | solution.py:120
  47.8 1.7 multiply_convert_fusion.2
  52.3 1.6 fusion.63
  53.9 3.0 bitcast_dynamic-update-slice_fusion.2
  57.1 1.7 multiply_convert_fusion.2
  63.2 3.1 bitcast_dynamic-update-slice_fusion.2
  66.4 1.7 multiply_convert_fusion.2
  72.5 3.1 bitcast_dynamic-update-slice_fusion.2
  75.7 1.7 multiply_convert_fusion.2
  81.7 3.0 bitcast_dynamic-update-slice_fusion.2
  84.9 13.5 %scatter_custom_fusion = f32[512,512]{1,0:T(8,128)S(1)} fusion(s32[2048]{0:T(1024)} %bitcast.107, f32[2048,512]{1,0:T(8,128)} %bitcast.108, f32[]{:T(128)} %constant.75.clone.1), kind=kCustom, calls=%fused_computation.35 | custom fusion | flops 1048576 | bytes 1049088 | tf_op jit(solution)/shard_map/scatter-add | solution.py:131
  99.4 13.2 %scatter_custom_fusion.1 = f32[24,512]{1,0:T(8,128)S(1)} fusion(s32[2048]{0:T(1024)S(1)} %bitcast.106, f32[2048,512]{1,0:T(8,128)} %bitcast.109, f32[]{:T(128)} %constant.75.clone.1), kind=kCustom, calls=%fused_computation.45 | custom fusion | flops 1048576 | bytes 49664 | tf_op jit(solution)/shard_map/scatter-add | solution.py:125
  112.6 4.8 %collective-permute-start.2 = (f32[8,512]{1,0:T(8,128)S(1)}, f32[8,512]{1,0:T(8,128)S(1)}, u32[]{:S(2)}, u32[]{:S(2)}) collective-permute-start(f32[8,512]{1,0:T(8,128)S(1)} %get-tuple-element.159), channel_id=1, source_target_pairs={{0,4},{4,8},{8,12},{12,16},{16,20},{20,24},{24,28},{1,5},{5,9},{9,... | collective-permute-start | bytes 49160 | tf_op jit(solution)/shard_map/ppermute | solution.py:27
  117.4 1.5 collective-permute-start.3
  118.9 3.8 %reduce_sum.81 = f32[512,512]{1,0:T(8,128)} reduce(f32[4,512,512]{2,1,0:T(8,128)} %get-tuple-element.73, f32[]{:T(128)} %constant.75.clone.1), dimensions={0}, to_apply=%region_15.16 | reduce | flops 786432 | bytes 5242884 | tf_op jit(solution)/shard_map/reduce_sum | solution.py:122
  124.4 2.3 fusion.14
  126.8 5.7 %all-reduce.1 = (f32[512]{0:T(512)S(1)}, f32[512]{0:T(512)S(1)}) all-reduce(f32[512]{0:T(512)S(1)} %reduce_sum.82, f32[512]{0:T(512)S(1)} %reduce_sum.83), channel_id=1, replica_groups=mesh['space'=8,'level'=4] {'level'}, use_global_device_ids=true, to_apply=%region_19.20 | all-reduce | flops 1024 | bytes 8192 | tf_op jit(solution)/shard_map/psum | solution.py:144
  134.4 62.2 %all-reduce.6.cloned.1.call-done = (f32[512,512]{0,1:T(8,128)}, f32[512,512]{1,0:T(8,128)}, f32[512,512]{1,0:T(8,128)}) async-done(((f32[512,512]{0,1:T(8,128)}, f32[512,512]{1,0:T(8,128)}, f32[512,512]{1,0:T(8,128)}), (f32[512,512]{0,1:T(8,128)}, f32[512,512]{1,0:T(8,128)}, f32[512,512]{1,0:T(8,128)})) %all-reduce.6.cloned.1.call-update) | async-done | bytes 3145744 | tf_op jit(solution)/shard_map/psum | solution.py:144
  196.6 130.5 %all-reduce.7 = (bf16[512,512]{0,1:T(8,128)(2,1)S(1)}, bf16[512,512]{1,0:T(8,128)(2,1)}, bf16[512,512]{1,0:T(8,128)(2,1)}, f32[512]{0:T(512)}, f32[512]{0:T(512)}) all-reduce(f32[512,512]{0,1:T(8,128)} %get-tuple-element.148, f32[512,512]{1,0:T(8,128)} %get-tuple-element.149, ...), channel_id=1, replica_groups=mesh['space'=8,'level'=4] {'space'}, use_global_device_ids=true, to_apply=%region_12.13 | all-reduce | flops 787456 | bytes 4726784 | tf_op jit(solution)/shard_map/psum | solution.py:143
  (103 shorter events, 28.0 us)
Async XLA Ops:
  7.2 13.3 %copy-start = (bf16[512,512]{1,0:T(8,128)(2,1)S(1)}, bf16[512,512]{1,0:T(8,128)(2,1)}, u32[]{:S(2)}) copy-start(bf16[512,512]{1,0:T(8,128)(2,1)} %param.15) | copy-start | bytes 1572868
  7.2 117.2 %reduce-scatter.2.cloned.1.call-start = ((), (), s32[]{:S(2)}) async-start(), calls=%async_computation.1 | async-start | bytes 655360 | tf_op jit(solution)/shard_map/reduce_scatter | solution.py:134
  8.5 30.0 %collective-permute-start.1 = (bf16[8,512]{1,0:T(8,128)(2,1)S(1)}, bf16[8,512]{1,0:T(8,128)(2,1)S(1)}, u32[]{:S(2)}, u32[]{:S(2)}) collective-permute-start(bf16[8,512]{1,0:T(8,128)(2,1)S(1)} %convolution_convert_fusion), channel_id=1, source_target_pairs={{4,0},{8,4},{12,8},{16,12},{20,16},{24,20},{28,24},{5,1},{9,5},{13... | collective-permute-start | bytes 24584 | tf_op jit(solution)/shard_map/ppermute | solution.py:17
  9.8 28.7 %collective-permute-start = (bf16[8,512]{1,0:T(8,128)(2,1)S(1)}, bf16[8,512]{1,0:T(8,128)(2,1)S(1)}, u32[]{:S(2)}, u32[]{:S(2)}) collective-permute-start(bf16[8,512]{1,0:T(8,128)(2,1)S(1)} %convolution_convert_fusion), channel_id=1, source_target_pairs={{0,4},{4,8},{8,12},{12,16},{16,20},{20,24},{24,28},{1,5},{5,9},{9,... | collective-permute-start | bytes 24584 | tf_op jit(solution)/shard_map/ppermute | solution.py:15
  38.5 9.2 %copy-start.1 = (bf16[512,512]{1,0:T(8,128)(2,1)S(1)}, bf16[512,512]{1,0:T(8,128)(2,1)}, u32[]{:S(2)}) copy-start(bf16[512,512]{1,0:T(8,128)(2,1)} %param.18) | copy-start | bytes 1572868
  38.5 9.2 %copy-start.5 = (f32[512]{0:T(512)S(1)}, f32[512]{0:T(512)}, u32[]{:S(2)}) copy-start(f32[512]{0:T(512)} %param.20) | copy-start | bytes 6148
  38.5 9.2 %copy-start.6 = (f32[512]{0:T(512)S(1)}, f32[512]{0:T(512)}, u32[]{:S(2)}) copy-start(f32[512]{0:T(512)} %param.19) | copy-start | bytes 6148
  84.9 38.2 %copy-start.7 = (bf16[1,8,512]{2,1,0:T(8,128)(2,1)S(1)}, bf16[1,8,512]{2,1,0:T(8,128)(2,1)}, u32[]{:S(2)}) copy-start(bf16[1,8,512]{2,1,0:T(8,128)(2,1)} %param.14) | copy-start | bytes 24580
  99.3 97.3 %all-reduce.6.cloned.1.call-start = ((), (), s32[]{:S(2)}) async-start(), calls=%async_computation.2 | async-start | bytes 6291456 | tf_op jit(solution)/shard_map/psum | solution.py:144
  112.6 10.1 %collective-permute-start.2 = (f32[8,512]{1,0:T(8,128)S(1)}, f32[8,512]{1,0:T(8,128)S(1)}, u32[]{:S(2)}, u32[]{:S(2)}) collective-permute-start(f32[8,512]{1,0:T(8,128)S(1)} %get-tuple-element.159), channel_id=1, source_target_pairs={{0,4},{4,8},{8,12},{12,16},{16,20},{20,24},{24,28},{1,5},{5,9},{9,... | collective-permute-start | bytes 49160 | tf_op jit(solution)/shard_map/ppermute | solution.py:27
  117.4 5.6 %collective-permute-start.3 = (f32[8,512]{1,0:T(8,128)S(1)}, f32[8,512]{1,0:T(8,128)S(1)}, u32[]{:S(2)}, u32[]{:S(2)}) collective-permute-start(f32[8,512]{1,0:T(8,128)S(1)} %get-tuple-element.160), channel_id=1, source_target_pairs={{4,0},{8,4},{12,8},{16,12},{20,16},{24,20},{28,24},{5,1},{9,5},{13... | collective-permute-start | bytes 49160 | tf_op jit(solution)/shard_map/ppermute | solution.py:27
  118.9 13.6 %copy-start.2 = (bf16[512,512]{1,0:T(8,128)(2,1)S(1)}, bf16[512,512]{1,0:T(8,128)(2,1)}, u32[]{:S(2)}) copy-start(bf16[512,512]{1,0:T(8,128)(2,1)} %param.16) | copy-start | bytes 1572868
  122.8 10.6 %copy-start.3 = (bf16[512,512]{1,0:T(8,128)(2,1)S(1)}, bf16[512,512]{1,0:T(8,128)(2,1)}, u32[]{:S(2)}) copy-start(bf16[512,512]{1,0:T(8,128)(2,1)} %param.17) | copy-start | bytes 1572868
  124.4 8.9 %copy-start.4 = (bf16[128,512]{1,0:T(8,128)(2,1)S(1)}, bf16[128,512]{1,0:T(8,128)(2,1)}, u32[]{:S(2)}) copy-start(bf16[128,512]{1,0:T(8,128)(2,1)} %reduce-scatter.2.cloned.1.call-done) | copy-start | bytes 393220
Sparse Core Ops, SparseCore 0:
  99.4 23.2 reduce-scatter.1
  126.9 69.6 all-reduce.5
